TPU v7x, 32 devices: a whole 2x2x4 slice. The times are simulated.
32 devices in a mesh: dp: 8 (over y, x, core), tensor: 4 (over z).
Axes of the slice: x: 2, y: 2, z: 4, core: 2. Of those that a mesh axis runs over, the one named last changes fastest.
Arguments:
- tokens: bfloat16 [2048, 4096], P(('dp', 'tensor')), may hold values from -6 to 6
- gate_weight: bfloat16 [4096, 3584], P('dp', 'tensor'), may hold values from -0.09375 to 0.09375
- up_weight: bfloat16 [4096, 3584], P('dp', 'tensor'), may hold values from -0.09375 to 0.09375
- hidden_cotangent: bfloat16 [2048, 3584], P('dp', 'tensor'), may hold values from -1.5 to 1.5
Outputs:
- hidden: bfloat16 [2048, 3584], P('dp', 'tensor')
- grad_tokens: bfloat16 [2048, 4096], P(('dp', 'tensor'))
- grad_gate: bfloat16 [4096, 3584], P('dp', 'tensor')
- grad_up: bfloat16 [4096, 3584], P('dp', 'tensor')
All inputs are finite; a program needn't handle non-finite values.
Results may differ from a plain program's by a relative error of at most 0.023.
Values may be sent and summed in bfloat16 or wider, within the bound.
No kernel may reach another device: no remote copies, remote signals or barrier semaphores. Data moves between devices by JAX's collectives and lax.ppermute only.
A program may use at most 64 MiB of HBM per device.

v0:
```python
import jax
import jax.numpy as jnp
from jax import lax
from jax.sharding import PartitionSpec as P


def swiglu_parts(gate_pre, up_pre, cotangent):
    sigmoid_val = jax.nn.sigmoid(gate_pre)
    activation = gate_pre * sigmoid_val
    hidden = (activation * up_pre).astype(jnp.bfloat16)
    upstream = cotangent.astype(jnp.float32)
    slope = sigmoid_val * (1.0 + gate_pre * (1.0 - sigmoid_val))
    grad_gate_pre = (upstream * up_pre * slope).astype(jnp.bfloat16)
    grad_up_pre = (upstream * activation).astype(jnp.bfloat16)
    return (hidden, grad_gate_pre, grad_up_pre)


def body(tokens, gate_weight, up_weight, hidden_cotangent):
    width = gate_weight.shape[1]
    gathered = lax.all_gather(tokens, "tensor", axis=0, tiled=True)
    columns = lax.all_to_all(gathered, "dp", split_axis=1, concat_axis=0, tiled=True)
    joined_weight = jnp.concatenate([gate_weight, up_weight], axis=1)
    both_pre = lax.psum_scatter(
        jnp.dot(columns, joined_weight, preferred_element_type=jnp.float32).astype(jnp.bfloat16),
        "dp",
        scatter_dimension=0,
        tiled=True,
    ).astype(jnp.float32)
    gate_pre = both_pre[:, :width]
    up_pre = both_pre[:, width:]
    hidden, grad_gate_pre, grad_up_pre = swiglu_parts(gate_pre, up_pre, hidden_cotangent)
    every_gate, every_up = (
        lax.all_gather(grad_gate_pre, "dp", axis=0, tiled=True),
        lax.all_gather(grad_up_pre, "dp", axis=0, tiled=True),
    )
    partial_input = jnp.einsum(
        "tf,df->td", every_gate, gate_weight, preferred_element_type=jnp.float32
    )
    partial_input = partial_input + jnp.einsum(
        "tf,df->td", every_up, up_weight, preferred_element_type=jnp.float32
    )
    regrouped = lax.all_to_all(
        partial_input.astype(jnp.bfloat16), "dp", split_axis=0, concat_axis=1, tiled=True
    ).astype(partial_input.dtype)
    input_rows = lax.psum_scatter(
        regrouped.astype(jnp.bfloat16), "tensor", scatter_dimension=0, tiled=True
    )
    groups = lax.axis_size("dp")
    group_rows = gathered.shape[0]
    joined_grad = jnp.concatenate([every_gate, every_up], axis=1)
    token_blocks = columns.reshape(groups, group_rows, columns.shape[1])
    grad_blocks = joined_grad.reshape(groups, group_rows, 2 * width)
    terms = jnp.einsum(
        "kgd,kgf->kdf", token_blocks, grad_blocks, preferred_element_type=jnp.float32
    )
    terms = lax.optimization_barrier(terms.astype(jnp.bfloat16)).astype(jnp.float32)
    weight_total = jnp.sum(terms, axis=0)
    grad_gate = weight_total[:, :width].astype(jnp.bfloat16)
    grad_up = weight_total[:, width:].astype(jnp.bfloat16)
    return (hidden, input_rows, grad_gate, grad_up)


def solution(mesh):
    placed = (P(("dp", "tensor"), None), P("dp", "tensor"), P("dp", "tensor"), P("dp", "tensor"))
    return jax.shard_map(
        body,
        mesh=mesh,
        in_specs=placed,
        out_specs=(
            P("dp", "tensor"),
            P(("dp", "tensor"), None),
            P("dp", "tensor"),
            P("dp", "tensor"),
        ),
        check_vma=False,
    )
```

profile of v0, /device:TPU:0, one launch (start us, length us, event | category | flops | bytes accessed | tf_op | source)
XLA Modules:
  0.0 325.4 jit_solution(14604213847612209496)
XLA Ops:
  7.2 0.0 all-gather.4.cloned.1.call-start
  7.2 0.7 all-gather.4.cloned.1.call-update
  7.9 0.0 reduce-scatter.3.cloned.1.call-start
  7.9 50.0 %all-gather.4.cloned.1.call-done = bf16[256,4096]{1,0:T(8,128)(2,1)} async-done(((bf16[64,4096]{1,0:T(8,128)(2,1)}), bf16[256,4096]{1,0:T(8,128)(2,1)}) %all-gather.4.cloned.1.call-update) | async-done | bytes 2097168 | tf_op jit(solution)/shard_map/all_gather | solution.py:20
  58.0 3.3 %copy.18 = bf16[256,4096]{0,1:T(8,128)(2,1)S(1)} copy(bf16[256,4096]{1,0:T(8,128)(2,1)} %all-gather.4.cloned.1.call-done) | data formatting | bytes 4194304 | tf_op jit(solution)/shard_map/all_gather | solution.py:20
  61.2 0.0 copy-start.1
  61.2 2.4 copy.19
  63.7 0.0 copy-start.2
  63.7 30.3 %all_to_all.38 = bf16[256,8,512]{2,0,1:T(8,128)(2,1)S(1)} all-to-all(bf16[256,8,512]{2,0,1:T(8,128)(2,1)} %copy.19), channel_id=1, replica_groups=mesh['dp'=8,'tensor'=4] {'dp'}, dimensions={1} | all-to-all | bytes 4194304 | tf_op jit(solution)/shard_map/all_to_all | solution.py:21
  94.0 0.0 copy-done.1
  94.0 0.0 copy-done.2
  94.0 6.1 %fusion.2 = bf16[2048,1792]{0,1:T(8,128)(2,1)} fusion(bf16[2048,512]{1,0:T(8,128)(2,1)S(1)} %bitcast.24, bf16[512,896]{1,0:T(8,128)(2,1)S(1)} %copy-done.2, bf16[512,896]{1,0:T(8,128)(2,1)S(1)} %copy-done.1), kind=kOutput, calls=%fused_computation.5 | convolution fusion | flops 3765436416 | bytes 11272192 | tf_op jit(solution)/shard_map/dot_general | solution.py:24
  100.1 0.0 copy-start
  100.1 0.0 reduce-scatter.3.cloned.1.call-update
  100.2 0.0 all-gather.6.cloned.1.call-start
  100.2 0.9 copy-done
  101.1 0.2 copy.20
  101.4 62.7 %reduce-scatter.3.cloned.1.call-done = bf16[256,1792]{0,1:T(8,128)(2,1)} async-done(((bf16[2048,1792]{0,1:T(8,128)(2,1)}), bf16[256,1792]{0,1:T(8,128)(2,1)}) %reduce-scatter.3.cloned.1.call-update) | async-done | bytes 917520 | tf_op jit(solution)/shard_map/reduce_scatter | solution.py:23
  164.1 1.3 convert_element_type.39
  165.4 1.5 fusion.9
  166.9 0.0 all-gather.6.cloned.1.call-update
  166.9 0.0 all-gather.8.cloned.1.call-start
  167.0 0.5 all-gather.8.cloned.1.call-update
  167.5 0.0 copy-start.3
  167.5 0.0 reduce-scatter.5.cloned.1.call-start
  167.6 34.6 %all-gather.6.cloned.1.call-done = bf16[2048,896]{0,1:T(8,128)(2,1)} async-done(((bf16[256,896]{0,1:T(8,128)(2,1)}), bf16[2048,896]{0,1:T(8,128)(2,1)}) %all-gather.6.cloned.1.call-update) | async-done | bytes 3670032 | tf_op jit(solution)/shard_map/all_gather | solution.py:33
  202.1 6.6 %fusion.13 = f32[2048,512]{1,0:T(8,128)} fusion(bf16[2048,896]{0,1:T(8,128)(2,1)} %all-gather.6.cloned.1.call-done, bf16[512,896]{1,0:T(8,128)(2,1)} %param.5), kind=kOutput, calls=%fused_computation.21 | convolution fusion | flops 1879048192 | bytes 8781824 | tf_op jit(solution)/shard_map/tf,df->td/dot_general | solution.py:36
  208.8 30.7 %all-gather.8.cloned.1.call-done = bf16[2048,896]{0,1:T(8,128)(2,1)} async-done(((bf16[256,896]{0,1:T(8,128)(2,1)}), bf16[2048,896]{0,1:T(8,128)(2,1)}) %all-gather.8.cloned.1.call-update) | async-done | bytes 3670032 | tf_op jit(solution)/shard_map/all_gather | solution.py:34
  239.5 0.0 copy-done.3
  239.5 5.7 %add_convert_fusion = bf16[2048,512]{1,0:T(8,128)(2,1)S(1)} fusion(f32[2048,512]{1,0:T(8,128)} %fusion.13, bf16[2048,896]{0,1:T(8,128)(2,1)} %all-gather.8.cloned.1.call-done, bf16[512,896]{1,0:T(8,128)(2,1)S(1)} %copy-done.3), kind=kOutput, calls=%fused_computation.6 | convolution fusion | flops 1881145344 | bytes 10878976 | tf_op jit(solution)/shard_map/tf,df->td/dot_general | solution.py:39
  245.2 29.1 %all_to_all.39 = bf16[8,256,512]{2,1,0:T(8,128)(2,1)S(1)} all-to-all(bf16[8,256,512]{2,1,0:T(8,128)(2,1)S(1)} %bitcast.28), channel_id=1, replica_groups=mesh['dp'=8,'tensor'=4] {'dp'}, dimensions={0} | all-to-all | bytes 4194304 | tf_op jit(solution)/shard_map/all_to_all | solution.py:42
  274.3 1.6 copy.27
  276.0 0.0 reduce-scatter.5.cloned.1.call-update
  276.0 1.0 copy.23
  277.0 7.5 %pad_maximum_fusion = bf16[2048,1792]{0,1:T(8,128)(2,1)} fusion(bf16[2048,896]{0,1:T(8,128)(2,1)} %all-gather.8.cloned.1.call-done, bf16[2048,896]{0,1:T(8,128)(2,1)} %all-gather.6.cloned.1.call-done), kind=kLoop, calls=%fused_computation.4 | loop fusion | flops 14680064 | bytes 14680064 | tf_op jit(solution)/shard_map/concatenate | solution.py:50
  284.5 10.4 %convert_bitcast_fusion = bf16[8,512,1792]{1,2,0:T(8,128)(2,1)} fusion(bf16[224,8,8,256]{3,2,1,0:T(8,128)(2,1)} %bitcast.23, bf16[256,8,512]{2,0,1:T(8,128)(2,1)S(1)} %all_to_all.38), kind=kOutput, calls=%fused_computation | convolution fusion | flops 3765436416 | bytes 24117248 | tf_op jit(solution)/shard_map/kgd,kgf->kdf/dot_general | solution.py:53
  294.9 8.6 %reduce = bf16[512,1792]{0,1:T(8,128)(2,1)S(1)} reduce(bf16[8,512,1792]{1,2,0:T(8,128)(2,1)} %convert_bitcast_fusion, bf16[]{:T(256)} %constant.4), dimensions={0}, to_apply=%region_2.0.clone | reduce | flops 6422528 | bytes 16515074 | tf_op jit(solution)/shard_map/reduce_sum | solution.py:57
  303.5 1.0 fusion.12
  304.6 2.2 copy.25
  306.8 1.3 copy.24
  308.1 10.8 %reduce-scatter.5.cloned.1.call-done = bf16[64,4096]{1,0:T(8,128)(2,1)} async-done(((bf16[256,4096]{1,0:T(8,128)(2,1)}), bf16[64,4096]{1,0:T(8,128)(2,1)}) %reduce-scatter.5.cloned.1.call-update) | async-done | bytes 524304 | tf_op jit(solution)/shard_map/reduce_scatter | solution.py:45
Async XLA Ops:
  7.2 50.8 %all-gather.4.cloned.1.call-start = ((), (), s32[]{:S(2)}) async-start(), calls=%async_computation.4 | async-start | bytes 2621440 | tf_op jit(solution)/shard_map/all_gather | solution.py:20
  7.9 156.2 %reduce-scatter.3.cloned.1.call-start = ((), (), s32[]{:S(2)}) async-start(), calls=%async_computation.5 | async-start | bytes 8257536 | tf_op jit(solution)/shard_map/reduce_scatter | solution.py:23
  61.2 32.8 %copy-start.1 = (bf16[512,896]{1,0:T(8,128)(2,1)S(1)}, bf16[512,896]{1,0:T(8,128)(2,1)}, u32[]{:S(2)}) copy-start(bf16[512,896]{1,0:T(8,128)(2,1)} %param.5) | copy-start | bytes 2752516
  63.7 30.4 %copy-start.2 = (bf16[512,896]{1,0:T(8,128)(2,1)S(1)}, bf16[512,896]{1,0:T(8,128)(2,1)}, u32[]{:S(2)}) copy-start(bf16[512,896]{1,0:T(8,128)(2,1)} %param.6) | copy-start | bytes 2752516
  100.1 1.0 copy-start
  100.2 102.0 %all-gather.6.cloned.1.call-start = ((), (), s32[]{:S(2)}) async-start(), calls=%async_computation.6 | async-start | bytes 4128768 | tf_op jit(solution)/shard_map/all_gather | solution.py:33
  166.9 72.6 %all-gather.8.cloned.1.call-start = ((), (), s32[]{:S(2)}) async-start(), calls=%async_computation.7 | async-start | bytes 4128768 | tf_op jit(solution)/shard_map/all_gather | solution.py:34
  167.5 72.0 %copy-start.3 = (bf16[512,896]{1,0:T(8,128)(2,1)S(1)}, bf16[512,896]{1,0:T(8,128)(2,1)}, u32[]{:S(2)}) copy-start(bf16[512,896]{1,0:T(8,128)(2,1)} %param.6) | copy-start | bytes 2752516
  167.5 151.4 %reduce-scatter.5.cloned.1.call-start = ((), (), s32[]{:S(2)}) async-start(), calls=%async_computation.8 | async-start | bytes 2621440 | tf_op jit(solution)/shard_map/reduce_scatter | solution.py:45
Sparse Core Ops, SparseCore 0:
  9.5 48.3 all-gather.3
  100.3 63.7 reduce-scatter.2
  167.1 35.0 all-gather.5
  204.4 35.0 all-gather.7
  276.1 42.7 reduce-scatter.4
where the time goes:
time: 326 us; the launch traced here: 325 us
  waiting for transfers between devices  190 us (58%)
  blocking collectives  59.5 us (18%)
  matrix products  28.9 us (9%)
  other arithmetic  18.9 us (6%)
  local copies, waits for them, and re-layouts  14 us (4%)
  between operations  13.8 us (4%)
    reduce_scatter x1, waiting for transfers between devices, body(): lax.psum_scatter(jnp.dot(columns, joined_weight, preferred_element_type=j...  62.7 us
    all_gather x1, waiting for transfers between devices, body(): gathered = lax.all_gather(tokens, 'tensor', axis=0, tiled=True)  50 us
    all_gather x1, waiting for transfers between devices, body(): lax.all_gather(grad_gate_pre, 'dp', axis=0, tiled=True)  34.6 us
    all_gather x1, waiting for transfers between devices, body(): lax.all_gather(grad_up_pre, 'dp', axis=0, tiled=True)  30.7 us
    all_to_all x1, blocking collectives, body(): lax.all_to_all(gathered, 'dp', split_axis=1, concat_axis=0, tiled=True)  30.3 us
    all_to_all x1, blocking collectives, body(): lax.all_to_all(partial_input.astype(jnp.bfloat16), 'dp', split_axis=0, co...  29.1 us
    reduce_scatter x1, waiting for transfers between devices, body(): lax.psum_scatter(regrouped.astype(jnp.bfloat16), 'tensor', scatter_dimens...  10.8 us
    dot_general x1, matrix products, body(): jnp.einsum('kgd,kgf->kdf', token_blocks, grad_blocks, preferred_element_t...  10.4 us
  transfers between devices with their start and end apart: 5, of which 5 were waited for; matrix products, arithmetic and copies ran while one was open for 12% of the time, Pallas kernels for 0%

commit v1 on v0

--- a/solution.py
+++ b/solution.py
@@ -17,7 +17,9 @@
 
 def body(tokens, gate_weight, up_weight, hidden_cotangent):
     width = gate_weight.shape[1]
-    gathered = lax.all_gather(tokens, "tensor", axis=0, tiled=True)
+    gathered = jnp.concatenate(
+        lax.all_to_all(jnp.stack([tokens] * lax.axis_size("tensor")), "tensor", 0, 0), axis=0
+    )
     columns = lax.all_to_all(gathered, "dp", split_axis=1, concat_axis=0, tiled=True)
     joined_weight = jnp.concatenate([gate_weight, up_weight], axis=1)
     both_pre = lax.psum_scatter(

time: 326 us -> 327 us (level)
  blocking collectives: 59.5 us -> 114 us
  waiting for transfers between devices: 190 us -> 140 us
    all_to_all x0 -> x1, blocking collectives: none -> 54.3 us  [body(): lax.all_to_all(jnp.stack([tokens] * lax.axis_size('tensor')), 'tensor', 0...]
    all_gather x1 -> x0, waiting for transfers between devices: 50 us -> none  [body(): gathered = lax.all_gather(tokens, 'tensor', axis=0, tiled=True)]
  transfers between devices with their start and end apart: 5 -> 4, of which waited for: 5 -> 4; matrix products, arithmetic and copies ran while one was open for 12% -> 12% of each run, Pallas kernels for 0% -> 0%
where the time goes in v1:
time: 327 us; the launch traced here: 326 us
  waiting for transfers between devices  140 us (43%)
  blocking collectives  114 us (35%)
  matrix products  29 us (9%)
  other arithmetic  18.9 us (6%)
  between operations  13.8 us (4%)
  local copies, waits for them, and re-layouts  11.1 us (3%)
    reduce_scatter x1, waiting for transfers between devices, body(): lax.psum_scatter(jnp.dot(columns, joined_weight, preferred_element_type=j...  63.1 us
    all_to_all x1, blocking collectives, body(): lax.all_to_all(jnp.stack([tokens] * lax.axis_size('tensor')), 'tensor', 0...  54.3 us
    all_gather x1, waiting for transfers between devices, body(): lax.all_gather(grad_gate_pre, 'dp', axis=0, tiled=True)  34.4 us
    all_gather x1, waiting for transfers between devices, body(): lax.all_gather(grad_up_pre, 'dp', axis=0, tiled=True)  30.9 us
    all_to_all x1, blocking collectives, body(): lax.all_to_all(gathered, 'dp', split_axis=1, concat_axis=0, tiled=True)  30.1 us
    all_to_all x1, blocking collectives, body(): lax.all_to_all(partial_input.astype(jnp.bfloat16), 'dp', split_axis=0, co...  29.1 us
    reduce_scatter x1, waiting for transfers between devices, body(): lax.psum_scatter(regrouped.astype(jnp.bfloat16), 'tensor', scatter_dimens...  10.8 us
    dot_general x1, matrix products, body(): jnp.einsum('kgd,kgf->kdf', token_blocks, grad_blocks, preferred_element_t...  10.4 us
  transfers between devices with their start and end apart: 4, of which 4 were waited for; matrix products, arithmetic and copies ran while one was open for 12% of the time, Pallas kernels for 0%

profile of v1, /device:TPU:0, one launch (start us, length us, event | category | flops | bytes accessed | tf_op | source)
XLA Modules:
  0.0 326.5 jit_solution(6914392206026634413)
XLA Ops:
  7.2 0.0 reduce-scatter.3.cloned.1.call-start
  7.2 1.3 stack.2
  8.5 54.3 %all_to_all.43 = bf16[4,64,4096]{2,1,0:T(8,128)(2,1)S(1)} all-to-all(bf16[4,64,4096]{2,1,0:T(8,128)(2,1)S(1)} %stack.2), channel_id=1, replica_groups=mesh['dp'=8,'tensor'=4] {'tensor'}, dimensions={0} | all-to-all | bytes 4194304 | tf_op jit(solution)/shard_map/all_to_all | solution.py:21
  62.8 0.9 copy.26
  63.7 0.0 copy-start.1
  63.7 0.0 copy-start.2
  63.8 0.7 copy.17
  64.4 30.1 %all_to_all.44 = bf16[256,8,512]{2,0,1:T(8,128)(2,1)S(1)} all-to-all(bf16[256,8,512]{2,0,1:T(8,128)(2,1)S(1)} %copy.17), channel_id=1, replica_groups=mesh['dp'=8,'tensor'=4] {'dp'}, dimensions={1} | all-to-all | bytes 4194304 | tf_op jit(solution)/shard_map/all_to_all | solution.py:23
  94.5 0.0 copy-done.1
  94.5 0.0 copy-done.2
  94.5 6.2 %fusion.2 = bf16[2048,1792]{0,1:T(8,128)(2,1)} fusion(bf16[2048,512]{1,0:T(8,128)(2,1)S(1)} %bitcast.26, bf16[512,896]{1,0:T(8,128)(2,1)S(1)} %copy-done.2, bf16[512,896]{1,0:T(8,128)(2,1)S(1)} %copy-done.1), kind=kOutput, calls=%fused_computation.5 | convolution fusion | flops 3765436416 | bytes 11272192 | tf_op jit(solution)/shard_map/dot_general | solution.py:26
  100.7 0.0 copy-start
  100.7 0.0 reduce-scatter.3.cloned.1.call-update
  100.7 0.0 all-gather.3.cloned.1.call-start
  100.8 0.9 copy-done
  101.7 0.2 copy.18
  101.9 63.1 %reduce-scatter.3.cloned.1.call-done = bf16[256,1792]{0,1:T(8,128)(2,1)} async-done(((bf16[2048,1792]{0,1:T(8,128)(2,1)}), bf16[256,1792]{0,1:T(8,128)(2,1)}) %reduce-scatter.3.cloned.1.call-update) | async-done | bytes 917520 | tf_op jit(solution)/shard_map/reduce_scatter | solution.py:25
  165.0 1.3 convert_element_type.39
  166.4 1.5 fusion.9
  167.9 0.0 all-gather.3.cloned.1.call-update
  167.9 0.0 all-gather.5.cloned.1.call-start
  167.9 0.7 all-gather.5.cloned.1.call-update
  168.6 0.0 copy-start.3
  168.6 0.0 reduce-scatter.5.cloned.1.call-start
  168.7 34.4 %all-gather.3.cloned.1.call-done = bf16[2048,896]{0,1:T(8,128)(2,1)} async-done(((bf16[256,896]{0,1:T(8,128)(2,1)}), bf16[2048,896]{0,1:T(8,128)(2,1)}) %all-gather.3.cloned.1.call-update) | async-done | bytes 3670032 | tf_op jit(solution)/shard_map/all_gather | solution.py:35
  203.1 6.6 %fusion.13 = f32[2048,512]{1,0:T(8,128)} fusion(bf16[2048,896]{0,1:T(8,128)(2,1)} %all-gather.3.cloned.1.call-done, bf16[512,896]{1,0:T(8,128)(2,1)} %param.5), kind=kOutput, calls=%fused_computation.21 | convolution fusion | flops 1879048192 | bytes 8781824 | tf_op jit(solution)/shard_map/tf,df->td/dot_general | solution.py:38
  209.7 30.9 %all-gather.5.cloned.1.call-done = bf16[2048,896]{0,1:T(8,128)(2,1)} async-done(((bf16[256,896]{0,1:T(8,128)(2,1)}), bf16[2048,896]{0,1:T(8,128)(2,1)}) %all-gather.5.cloned.1.call-update) | async-done | bytes 3670032 | tf_op jit(solution)/shard_map/all_gather | solution.py:36
  240.6 0.0 copy-done.3
  240.6 5.7 %add_convert_fusion = bf16[2048,512]{1,0:T(8,128)(2,1)S(1)} fusion(f32[2048,512]{1,0:T(8,128)} %fusion.13, bf16[2048,896]{0,1:T(8,128)(2,1)} %all-gather.5.cloned.1.call-done, bf16[512,896]{1,0:T(8,128)(2,1)S(1)} %copy-done.3), kind=kOutput, calls=%fused_computation.6 | convolution fusion | flops 1881145344 | bytes 10878976 | tf_op jit(solution)/shard_map/tf,df->td/dot_general | solution.py:41
  246.3 29.1 %all_to_all.45 = bf16[8,256,512]{2,1,0:T(8,128)(2,1)S(1)} all-to-all(bf16[8,256,512]{2,1,0:T(8,128)(2,1)S(1)} %bitcast.31), channel_id=1, replica_groups=mesh['dp'=8,'tensor'=4] {'dp'}, dimensions={0} | all-to-all | bytes 4194304 | tf_op jit(solution)/shard_map/all_to_all | solution.py:44
  275.4 1.6 copy.25
  277.0 0.0 reduce-scatter.5.cloned.1.call-update
  277.1 1.0 copy.21
  278.0 7.5 %pad_maximum_fusion = bf16[2048,1792]{0,1:T(8,128)(2,1)} fusion(bf16[2048,896]{0,1:T(8,128)(2,1)} %all-gather.5.cloned.1.call-done, bf16[2048,896]{0,1:T(8,128)(2,1)} %all-gather.3.cloned.1.call-done), kind=kLoop, calls=%fused_computation.4 | loop fusion | flops 14680064 | bytes 14680064 | tf_op jit(solution)/shard_map/concatenate | solution.py:52
  285.5 10.4 %convert_bitcast_fusion = bf16[8,512,1792]{1,2,0:T(8,128)(2,1)} fusion(bf16[224,8,8,256]{3,2,1,0:T(8,128)(2,1)} %bitcast.25, bf16[256,8,512]{2,0,1:T(8,128)(2,1)S(1)} %all_to_all.44), kind=kOutput, calls=%fused_computation | convolution fusion | flops 3765436416 | bytes 24117248 | tf_op jit(solution)/shard_map/kgd,kgf->kdf/dot_general | solution.py:55
  295.9 8.6 %reduce = bf16[512,1792]{0,1:T(8,128)(2,1)S(1)} reduce(bf16[8,512,1792]{1,2,0:T(8,128)(2,1)} %convert_bitcast_fusion, bf16[]{:T(256)} %constant.4), dimensions={0}, to_apply=%region_2.0.clone | reduce | flops 6422528 | bytes 16515074 | tf_op jit(solution)/shard_map/reduce_sum | solution.py:59
  304.6 1.0 fusion.12
  305.6 2.2 copy.23
  307.8 1.3 copy.22
  309.1 10.8 %reduce-scatter.5.cloned.1.call-done = bf16[64,4096]{1,0:T(8,128)(2,1)} async-done(((bf16[256,4096]{1,0:T(8,128)(2,1)}), bf16[64,4096]{1,0:T(8,128)(2,1)}) %reduce-scatter.5.cloned.1.call-update) | async-done | bytes 524304 | tf_op jit(solution)/shard_map/reduce_scatter | solution.py:47
Async XLA Ops:
  7.2 157.9 %reduce-scatter.3.cloned.1.call-start = ((), (), s32[]{:S(2)}) async-start(), calls=%async_computation.5 | async-start | bytes 8257536 | tf_op jit(solution)/shard_map/reduce_scatter | solution.py:25
  63.7 30.8 %copy-start.1 = (bf16[512,896]{1,0:T(8,128)(2,1)S(1)}, bf16[512,896]{1,0:T(8,128)(2,1)}, u32[]{:S(2)}) copy-start(bf16[512,896]{1,0:T(8,128)(2,1)} %param.5) | copy-start | bytes 2752516
  63.7 30.8 %copy-start.2 = (bf16[512,896]{1,0:T(8,128)(2,1)S(1)}, bf16[512,896]{1,0:T(8,128)(2,1)}, u32[]{:S(2)}) copy-start(bf16[512,896]{1,0:T(8,128)(2,1)} %param.6) | copy-start | bytes 2752516
  100.7 1.0 copy-start
  100.7 102.3 %all-gather.3.cloned.1.call-start = ((), (), s32[]{:S(2)}) async-start(), calls=%async_computation.6 | async-start | bytes 4128768 | tf_op jit(solution)/shard_map/all_gather | solution.py:35
  167.9 72.7 %all-gather.5.cloned.1.call-start = ((), (), s32[]{:S(2)}) async-start(), calls=%async_computation.7 | async-start | bytes 4128768 | tf_op jit(solution)/shard_map/all_gather | solution.py:36
  168.6 72.0 %copy-start.3 = (bf16[512,896]{1,0:T(8,128)(2,1)S(1)}, bf16[512,896]{1,0:T(8,128)(2,1)}, u32[]{:S(2)}) copy-start(bf16[512,896]{1,0:T(8,128)(2,1)} %param.6) | copy-start | bytes 2752516
  168.6 151.3 %reduce-scatter.5.cloned.1.call-start = ((), (), s32[]{:S(2)}) async-start(), calls=%async_computation.8 | async-start | bytes 2621440 | tf_op jit(solution)/shard_map/reduce_scatter | solution.py:47
Sparse Core Ops, SparseCore 0:
  100.9 64.1 reduce-scatter.2
  168.0 35.0 all-gather.2
  205.5 35.0 all-gather.4
  277.2 42.6 reduce-scatter.4
